TPU v7x, 32 devices: a whole 2x2x4 slice. The times are simulated.
32 devices in a mesh: row: 8 (over z, x), col: 4 (over y, core).
Axes of the slice: x: 2, y: 2, z: 4, core: 2. Of those that a mesh axis runs over, the one named last changes fastest.
Arguments:
- front_pivot: float32 [64, 128, 128], P('col', 'row'), may hold values from -256 to 256, as said below
- front_update: float32 [64, 640, 768], P('col', 'row'), may hold values from -12 to 12, as said below
- child_blocks: float32 [64, 2, 512, 512], P('col', None, 'row'), may hold values from -0.5 to 0.5, as said below
- child_map: int32 [64, 2, 512], P('col'), may hold values from -1 to 767, as said below
Outputs:
- lhat: float32 [64, 640, 128], P('col', 'row')
- schur: float32 [64, 640, 640], P('col', 'row')
- negative_share: float32 [], replicated
Inputs may be any that keep to these rules, and one draw needn't show every extreme that they name: `front_pivot`: symmetric in its last two dimensions. With both children's entries added, the pivot block of every front has an LDL^T factorization without pivoting whose pivots have magnitudes 4 to 40. `front_update`: the last 640 columns of each front form a symmetric matrix. `child_blocks`: symmetric in its last two dimensions. child_map[f, c, i] is the row and column of front f's assembled matrix that row and column i of child c go to, or -1 for padding. A child's entries of 0 or more are distinct, come before its padding, and number at least 385, and more than half of 512. Parent row p is held by grid row p // 16 if p < 128, else by (p - 128) // 80. Of the 64 rows i of a child with the same i // 64, at most 16 go to rows held by any one grid row, and every child reaches that bound.
All inputs are finite; a program needn't handle non-finite values.
Results may differ from a plain program's by a relative error of at most 0.0003.
Values sent between devices are 32-bit elements; how exact they have to be, the bound alone decides.
No kernel may reach another device: no remote copies, remote signals or barrier semaphores. Data moves between devices by JAX's collectives and lax.ppermute only.
A program may use at most 64 MiB of HBM per device.

v0:
```python
import jax
import jax.numpy as jnp
from jax import lax
from jax.sharding import PartitionSpec as P

highest = lax.Precision.HIGHEST


def factor(blocks):
    fronts, count = (blocks.shape[0], blocks.shape[-1])
    panel_width = 8
    index = jnp.arange(count, dtype=jnp.int32)

    def panel_step(panel, carry):
        current, lower, pivots = carry
        start = panel * panel_width
        strip = lax.dynamic_slice_in_dim(current, start, panel_width, 2)
        columns = []
        values = []
        for inner in range(panel_width):
            place = start + inner
            leading = lax.dynamic_index_in_dim(strip, place, 1, keepdims=False)
            pivot = leading[:, inner]
            below = index[None, :] > place
            column = strip[:, :, inner]
            multiplier = jnp.where(below, column / pivot[:, None], jnp.zeros_like(column))
            strip = strip - multiplier[:, :, None] * leading[:, None, :]
            columns.append(multiplier)
            values.append(pivot)
        panel_lower = jnp.stack(columns, axis=2)
        panel_pivots = jnp.stack(values, axis=1)
        lower = lax.dynamic_update_slice_in_dim(lower, panel_lower, start, 2)
        pivots = lax.dynamic_update_slice_in_dim(pivots, panel_pivots, start, 1)
        product = jnp.einsum(
            "fiw,fjw->fij", panel_lower * panel_pivots[:, None, :], panel_lower, precision=highest
        )
        later = index >= start + panel_width
        current = current - jnp.where(
            later[:, None] & later[None, :], product, jnp.zeros_like(product)
        )
        return (current, lower, pivots)

    start_state = (blocks, jnp.zeros_like(blocks), jnp.zeros((fronts, count), blocks.dtype))
    current, lower, pivots = lax.fori_loop(0, count // panel_width, panel_step, start_state)
    identity = jnp.eye(count, dtype=blocks.dtype)
    inverse = jax.vmap(
        lambda matrix: jax.scipy.linalg.solve_triangular(
            matrix, identity, lower=True, unit_diagonal=True
        )
    )(lower)
    return (inverse, pivots)


def local(front_pivot, front_update, child_blocks, child_map):
    row_count = lax.axis_size("row")
    my_row = lax.axis_index("row")
    fronts, pivot_rows, pivot_width = front_pivot.shape
    update_rows, width = (front_update.shape[1], front_update.shape[2])
    held, child_width = (child_blocks.shape[2], child_blocks.shape[3])
    capacity = 2 * held // row_count
    slot_count = row_count * capacity
    local_rows = pivot_rows + update_rows
    valid = child_map >= 0
    in_pivot = child_map < pivot_width
    owner = jnp.where(in_pivot, child_map // pivot_rows, (child_map - pivot_width) // update_rows)
    owner = jnp.where(valid, owner, row_count)
    target_row = jnp.where(
        in_pivot, child_map % pivot_rows, pivot_rows + (child_map - pivot_width) % update_rows
    )
    owner_hot = (owner[..., None] == jnp.arange(row_count, dtype=jnp.int32)).astype(jnp.int32)
    blocked = owner_hot.reshape(fronts, 2, row_count, held, row_count)
    earlier = jnp.cumsum(blocked, axis=3) - blocked
    rank = jnp.sum(earlier * blocked, axis=4).reshape(fronts, 2, child_width)
    position = jnp.arange(child_width, dtype=jnp.int32)
    slot = owner * capacity + rank
    arrival = (position // held)[None, None, :] * capacity + rank
    my_slot = lax.dynamic_slice_in_dim(slot, my_row * held, held, 2)
    my_valid = lax.dynamic_slice_in_dim(valid, my_row * held, held, 2)
    slot_range = jnp.arange(slot_count, dtype=jnp.int32)
    packing = (
        (my_slot[:, :, None, :] == slot_range[None, None, :, None]) & my_valid[:, :, None, :]
    ).astype(jnp.float32)
    outgoing = jnp.einsum("fcsq,fcqj->fcsj", packing, child_blocks, precision=highest)
    outgoing = outgoing.reshape(fronts, 2, row_count, capacity, child_width)
    incoming = lax.all_to_all(outgoing, "row", split_axis=2, concat_axis=2, tiled=True)
    incoming = incoming.reshape(fronts, 2, slot_count, child_width)
    mine = valid & (owner == my_row)
    row_hot = (
        (target_row[..., None] == jnp.arange(local_rows, dtype=jnp.int32)) & mine[..., None]
    ).astype(jnp.float32)
    arrival_hot = (arrival[..., None] == slot_range).astype(jnp.float32)
    placing = jnp.einsum("fcil,fcip->fclp", row_hot, arrival_hot, precision=highest)
    placed = jnp.einsum("fclp,fcpq->fclq", placing, incoming, precision=highest)
    column_range = jnp.arange(width, dtype=jnp.int32)

    def place_columns(inputs):
        rows_placed, indices = inputs
        column_hot = (indices[:, :, None] == column_range[None, None, :]).astype(jnp.float32)
        total = jnp.dot(
            rows_placed[0], column_hot[0], precision=highest, preferred_element_type=jnp.float32
        )
        return total + jnp.dot(
            rows_placed[1], column_hot[1], precision=highest, preferred_element_type=jnp.float32
        )

    added = lax.map(place_columns, (placed, child_map))
    pivot_local = front_pivot + added[:, :pivot_rows, :pivot_width]
    update_local = front_update + added[:, pivot_rows:, :]
    coupling = update_local[:, :, :pivot_width]
    trailing = update_local[:, :, pivot_width:]
    own_fronts = lax.all_to_all(pivot_local, "row", split_axis=0, concat_axis=1, tiled=True)
    own_inverse, own_pivots = factor(own_fronts)
    inverse, pivots = (
        lax.all_gather(own_inverse, "row", axis=0, tiled=True),
        lax.all_gather(own_pivots, "row", axis=0, tiled=True),
    )
    lhat = jnp.einsum("fik,fjk->fij", coupling, inverse, precision=highest)
    scaled = lhat / pivots[:, None, :]
    correction = jnp.einsum(
        "fik,fjk->fij", scaled, lax.all_gather(lhat, "row", axis=1, tiled=True), precision=highest
    )
    schur = trailing - correction
    negatives = jnp.sum(jnp.where(pivots < 0.0, 1.0, 0.0).astype(jnp.float32))
    total = lax.psum(negatives, "col")
    negative_share = total / (fronts * lax.axis_size("col") * pivot_width)
    return (lhat, schur, negative_share)


def solution(mesh):
    in_specs = (
        P("col", "row", None),
        P("col", "row", None),
        P("col", None, "row", None),
        P("col", None, None),
    )
    out_specs = (P("col", "row", None), P("col", "row", None), P())
    return jax.shard_map(local, mesh=mesh, in_specs=in_specs, out_specs=out_specs, check_vma=False)
```

profile of v0, /device:TPU:0, one launch (start us, length us, event | category | flops | bytes accessed | tf_op | source)
XLA Modules:
  0.0 599.0 jit_solution(478743614236139514)
XLA Ops:
  7.2 1.0 compare_and_fusion
  8.6 42.6 %fusion.18 = s32[16,2,8,64]{2,3,1,0:T(8,128)S(1)} fusion(s32[16,2,8,64]{2,3,1,0:T(8,128)S(1)} %copy.48), kind=kOutput, calls=%fused_computation.74 | output fusion | flops 9158656 | bytes 131072 | tf_op jit(solution)/shard_map/jit(cumsum)/reduce_window_sum | solution.py:72
  51.8 6.6 %fusion.27 = f32[16,2,128,512]{3,2,1,0:T(8,128)S(1)} fusion(f32[16,2,64,512]{3,2,1,0:T(8,128)} %param.10, s32[16,2,64]{2,1,0:T(2,128)S(1)} %copy.51, pred[16,2,64]{2,1,0:T(4,128)(4,1)S(1)} %copy.52), kind=kOutput, calls=%fused_computation.88 | convolution fusion | flops 1611137024 | bytes 12593152 | tf_op jit(solution)/shard_map/fcsq,fcqj->fcsj/dot_general | solution.py:83
  58.4 4.3 copy.53
  62.7 7.4 %all-to-all-start = ((f32[16,2,8,16,512]{4,3,1,0,2:T(8,128)}), f32[16,2,8,16,512]{4,3,1,0,2:T(8,128)}, u32[]{:S(2)}, u32[]{:S(2)}) async-start(f32[16,2,8,16,512]{4,3,1,0,2:T(8,128)} %copy.53), calls=%async_computation | async-start | bytes 16777216 | tf_op jit(solution)/shard_map/all_to_all | solution.py:85
  70.4 6.0 fusion.19
  76.3 176.9 %all-to-all-done = f32[16,2,8,16,512]{4,3,1,0,2:T(8,128)} async-done(((f32[16,2,8,16,512]{4,3,1,0,2:T(8,128)}), f32[16,2,8,16,512]{4,3,1,0,2:T(8,128)}, u32[]{:S(2)}, u32[]{:S(2)}) %all-to-all-start) | async-done | bytes 8388640 | tf_op jit(solution)/shard_map/all_to_all | solution.py:85
  253.3 4.4 copy.54
  257.7 7.6 %fusion.61 = f32[16,2,96,512]{3,2,1,0:T(8,128)} fusion(f32[16,2,96,128]{3,2,1,0:T(8,128)S(1)} %fusion.19, f32[16,2,128,512]{3,2,1,0:T(8,128)S(1)} %bitcast.85), kind=kOutput, calls=%fused_computation.148 | convolution fusion | flops 2415919104 | bytes 16252928 | tf_op jit(solution)/shard_map/fclp,fcpq->fclq/dot_general | solution.py:93
  265.3 69.4 %while.33 = (s32[]{:T(128)}, f32[16,96,768]{2,1,0:T(8,128)}, f32[16,2,96,512]{3,2,1,0:T(8,128)}, s32[16,2,512]{2,1,0:T(2,128)S(1)}, s32[]{:T(128)}, /*index=5*/s32[]{:T(128)}, s32[]{}) while((s32[]{:T(128)}, f32[16,96,768]{2,1,0:T(8,128)}, f32[16,2,96,512]{3,2,1,0:T(8,128)}, s32[16,2,512]{2,1,0:T(2,128)S(1)}, s32[]{:T(128)}, ...), condition=%wide.region_3.4_spmd.clone, body=%wide.region_2.3_spmd.clone.sunk | while | flops 906829824 | bytes 2864737 | solution.py:106
  265.3 0.5 iota_compare_fusion.29
  265.8 1.6 fusion.81
  267.4 2.3 fusion.82
  269.6 0.5 iota_compare_fusion.29
  270.1 1.6 fusion.81
  271.7 2.3 fusion.82
  273.9 0.5 iota_compare_fusion.29
  274.5 1.6 fusion.81
  276.0 2.3 fusion.82
  278.3 0.5 iota_compare_fusion.29
  278.8 1.6 fusion.81
  280.3 2.3 fusion.82
  282.6 0.5 iota_compare_fusion.29
  283.1 1.6 fusion.81
  284.7 2.3 fusion.82
  286.9 0.5 iota_compare_fusion.29
  287.4 1.6 fusion.81
  289.0 2.3 fusion.82
  291.3 0.5 iota_compare_fusion.29
  291.8 1.6 fusion.81
  293.3 2.3 fusion.82
  295.6 0.5 iota_compare_fusion.29
  296.1 1.6 fusion.81
  297.7 2.3 fusion.82
  300.5 1.6 fusion.81
  302.0 2.3 fusion.82
  304.8 1.6 fusion.81
  306.4 2.3 fusion.82
  309.2 1.6 fusion.81
  310.7 2.3 fusion.82
  313.5 1.6 fusion.81
  315.1 2.3 fusion.82
  317.8 1.6 fusion.81
  319.4 2.3 fusion.82
  322.2 1.6 fusion.81
  323.7 2.3 fusion.82
  326.5 1.6 fusion.81
  328.1 2.2 fusion.82
  330.8 1.6 fusion.81
  332.4 2.3 fusion.82
  334.7 1.6 slice_add_fusion.1
  336.2 3.6 all-to-all-start.1
  340.0 7.2 %all-to-all-done.1 = f32[16,16,128]{2,1,0:T(8,128)S(1)} async-done(((f32[16,16,128]{2,1,0:T(8,128)}), f32[16,16,128]{2,1,0:T(8,128)S(1)}, u32[]{:S(2)}, u32[]{:S(2)}) %all-to-all-start.1) | async-done | bytes 131104 | tf_op jit(solution)/shard_map/all_to_all | solution.py:111
  347.4 83.5 %while.34 = (s32[]{:T(128)}, f32[2,128,128]{1,2,0:T(8,128)S(1)}, f32[2,128,128]{1,2,0:T(8,128)S(1)}, f32[2,128]{1,0:T(2,128)S(1)}, s32[]{:T(128)}, /*index=5*/s3...) while((s32[]{:T(128)}, f32[2,128,128]{1,2,0:T(8,128)S(1)}, ...), condition=%wide.region_5.6_spmd.clone.clone, body=%wide.region_4.5_spmd.clone.clone.sunk | while | flops 3349669 | bytes 1026329 | solution.py:44
  431.0 19.7 %custom-call.4 = f32[2,1,128,128]{2,3,1,0:T(8,128)S(1)} custom-call(f32[2,1,128,128]{3,2,1,0:T(8,128)S(1)} %add_bitcast_fusion), custom_call_target="InvertDiagBlocksLowerTriangular" | custom-call | tf_op jit(solution)/shard_map/vmap(jit(_solve_triangular))/triangular_solve | solution.py:47
  450.7 1.0 fusion.35
  452.0 5.8 slice_add_fusion
  457.8 32.4 %all-gather.4.cloned.1.call-done = f32[16,128,128]{2,1,0:T(8,128)} async-done(((f32[2,128,128]{2,1,0:T(8,128)}), f32[16,128,128]{2,1,0:T(8,128)}) %all-gather.4.cloned.1.call-update) | async-done | bytes 1048592 | tf_op jit(solution)/shard_map/all_gather | solution.py:114
  490.1 4.4 fusion.29
  494.6 18.7 %all-gather = f32[8,2,128]{2,1,0:T(2,128)S(1)} all-gather(f32[1,2,128]{2,1,0:T(2,128)S(1)} %bitcast.118), channel_id=1, replica_groups=mesh['row'=8,'col'=4] {'row'}, dimensions={0}, use_global_device_ids=true | all-gather | bytes 9216 | tf_op jit(solution)/shard_map/all_gather | solution.py:115
  513.3 0.6 select_reduce_fusion
  513.9 6.7 %psum.7 = f32[]{:T(128)} all-reduce(f32[]{:T(128)} %select_reduce_fusion), channel_id=1, replica_groups=mesh['row'=8,'col'=4] {'col'}, use_global_device_ids=true, to_apply=%region_7.8 | all-reduce | flops 1 | bytes 8 | tf_op jit(solution)/shard_map/psum | solution.py:124
  521.2 58.1 %all-gather.6.cloned.1.call-done = f32[16,640,128]{2,1,0:T(8,128)} async-done(((f32[16,80,128]{2,1,0:T(8,128)}), f32[16,640,128]{2,1,0:T(8,128)}) %all-gather.6.cloned.1.call-update) | async-done | bytes 5242896 | tf_op jit(solution)/shard_map/all_gather | solution.py:120
  579.4 11.6 %slice_subtract_fusion = f32[16,80,640]{2,1,0:T(8,128)} fusion(f32[16,80,768]{2,1,0:T(8,128)} %slice_add_fusion, f32[16,640,128]{2,1,0:T(8,128)} %all-gather.6.cloned.1.call-done, f32[16,80,128]{2,1,0:T(8,128)} %fusion.29, f32[16,128]{1,0:T(8,128)S(1)} %bitcast.117), kind=kOutput, calls=%fused_computation.83 | convolution fusion | flops 1259274240 | bytes 12460032 | tf_op jit(solution)/shard_map/fik,fjk->fij/dot_general | solution.py:119
  (824 shorter events, 86.5 us)
Async XLA Ops:
  62.7 7.5 %copy-start = (s32[16,2,512]{2,1,0:T(2,128)S(1)}, s32[16,2,512]{2,1,0:T(2,128)}, u32[]{:S(2)}) copy-start(s32[16,2,512]{2,1,0:T(2,128)} %param.11) | copy-start | bytes 196612
  62.7 190.6 %all-to-all-start = ((f32[16,2,8,16,512]{4,3,1,0,2:T(8,128)}), f32[16,2,8,16,512]{4,3,1,0,2:T(8,128)}, u32[]{:S(2)}, u32[]{:S(2)}) async-start(f32[16,2,8,16,512]{4,3,1,0,2:T(8,128)} %copy.53), calls=%async_computation | async-start | bytes 16777216 | tf_op jit(solution)/shard_map/all_to_all | solution.py:85
  265.3 69.4 %copy-start.1 = (f32[16,16,128]{2,1,0:T(8,128)S(1)}, f32[16,16,128]{2,1,0:T(8,128)}, u32[]{:S(2)}) copy-start(f32[16,16,128]{2,1,0:T(8,128)} %param.8) | copy-start | bytes 393220
  336.2 11.0 %all-to-all-start.1 = ((f32[16,16,128]{2,1,0:T(8,128)}), f32[16,16,128]{2,1,0:T(8,128)S(1)}, u32[]{:S(2)}, u32[]{:S(2)}) async-start(f32[16,16,128]{2,1,0:T(8,128)} %slice_add_fusion.1), calls=%async_computation.1 | async-start | bytes 262144 | tf_op jit(solution)/shard_map/all_to_all | solution.py:111
  339.9 150.3 %all-gather.4.cloned.1.call-start = ((), (), s32[]{:S(2)}) async-start(), calls=%async_computation.2 | async-start | bytes 1179648 | tf_op jit(solution)/shard_map/all_gather | solution.py:114
  451.7 127.7 %all-gather.6.cloned.1.call-start = ((), (), s32[]{:S(2)}) async-start(), calls=%async_computation.3 | async-start | bytes 5898240 | tf_op jit(solution)/shard_map/all_gather | solution.py:120
Sparse Core Ops, SparseCore 0:
  451.8 38.2 all-gather.3
  494.7 84.6 all-gather.5
where the time goes:
time: 600 us; the launch traced here: 599 us
  waiting for transfers between devices  275 us (46%)
  matrix products  106 us (18%)
  other arithmetic  101 us (17%)
  local copies, waits for them, and re-layouts  62.1 us (10%)
  blocking collectives  25.4 us (4%)
  between operations  16 us (3%)
  starting transfers between devices  11.3 us (2%)
    all_to_all x1, waiting for transfers between devices, local(): lax.all_to_all(outgoing, 'row', split_axis=2, concat_axis=2, tiled=True)  177 us
    all_gather x1, waiting for transfers between devices, local(): lax.all_gather(lhat, 'row', axis=1, tiled=True)  58.1 us
    another operation x1, other arithmetic, local(): earlier = jnp.cumsum(blocked, axis=3) - blocked  42.6 us
    dot_general x16, matrix products, place_columns(): jnp.dot(rows_placed[0], column_hot[0], precision=highest, preferred_eleme...  36.3 us
    all_gather x1, waiting for transfers between devices, local(): lax.all_gather(own_inverse, 'row', axis=0, tiled=True)  32.4 us
    dot_general x16, matrix products, place_columns(): jnp.dot(rows_placed[1], column_hot[1], precision=highest, preferred_eleme...  24.8 us
    slice x128, local copies, waits for them, and re-layouts, panel_step(): pivot = leading[:, inner]  22.7 us
    dynamic_slice x128, local copies, waits for them, and re-layouts, panel_step(): leading = lax.dynamic_index_in_dim(strip, place, 1, keepdims=False)  20.2 us
  transfers between devices with their start and end apart: 4, of which 4 were waited for; matrix products, arithmetic and copies ran while one was open for 2% of the time, Pallas kernels for 0%

commit v1 on v0

--- a/solution.py
+++ b/solution.py
@@ -4,6 +4,12 @@
 from jax.sharding import PartitionSpec as P
 
 highest = lax.Precision.HIGHEST
+
+
+def trade_parts(x, name, split, join):
+    pieces = jnp.split(x, lax.axis_size(name), axis=split)
+    incoming = lax.all_to_all(jnp.stack(pieces), name, 0, 0)
+    return jnp.concatenate(incoming, axis=join)
 
 
 def factor(blocks):
@@ -82,7 +88,7 @@
     ).astype(jnp.float32)
     outgoing = jnp.einsum("fcsq,fcqj->fcsj", packing, child_blocks, precision=highest)
     outgoing = outgoing.reshape(fronts, 2, row_count, capacity, child_width)
-    incoming = lax.all_to_all(outgoing, "row", split_axis=2, concat_axis=2, tiled=True)
+    incoming = trade_parts(outgoing, "row", 2, 2)
     incoming = incoming.reshape(fronts, 2, slot_count, child_width)
     mine = valid & (owner == my_row)
     row_hot = (

time: 600 us -> 604 us (level)
    unnamed x5 -> x12, local copies, waits for them, and re-layouts: 0.1 us -> 7.63 us
where the time goes in v1:
time: 604 us; the launch traced here: 603 us
  waiting for transfers between devices  275 us (46%)
  matrix products  106 us (18%)
  other arithmetic  101 us (17%)
  local copies, waits for them, and re-layouts  66.4 us (11%)
  blocking collectives  25.4 us (4%)
  between operations  16 us (3%)
  starting transfers between devices  11.3 us (2%)
    all_to_all x1, waiting for transfers between devices, trade_parts(): incoming = lax.all_to_all(jnp.stack(pieces), name, 0, 0)  177 us
    all_gather x1, waiting for transfers between devices, local(): lax.all_gather(lhat, 'row', axis=1, tiled=True)  58.1 us
    another operation x1, other arithmetic, local(): earlier = jnp.cumsum(blocked, axis=3) - blocked  42.6 us
    dot_general x16, matrix products, place_columns(): jnp.dot(rows_placed[0], column_hot[0], precision=highest, preferred_eleme...  36.3 us
    all_gather x1, waiting for transfers between devices, local(): lax.all_gather(own_inverse, 'row', axis=0, tiled=True)  32.6 us
    dot_general x16, matrix products, place_columns(): jnp.dot(rows_placed[1], column_hot[1], precision=highest, preferred_eleme...  24.8 us
    slice x128, local copies, waits for them, and re-layouts, panel_step(): pivot = leading[:, inner]  22.7 us
    dynamic_slice x128, local copies, waits for them, and re-layouts, panel_step(): leading = lax.dynamic_index_in_dim(strip, place, 1, keepdims=False)  20.2 us
  transfers between devices with their start and end apart: 4, of which 4 were waited for; matrix products, arithmetic and copies ran while one was open for 2% of the time, Pallas kernels for 0%

profile of v1, /device:TPU:0, one launch (start us, length us, event | category | flops | bytes accessed | tf_op | source)
XLA Modules:
  0.0 603.1 jit_solution(8654890875188140657)
XLA Ops:
  7.2 1.0 compare_and_fusion
  8.6 42.6 %fusion.18 = s32[16,2,8,64]{2,3,1,0:T(8,128)S(1)} fusion(s32[16,2,8,64]{2,3,1,0:T(8,128)S(1)} %copy.78), kind=kOutput, calls=%fused_computation.74 | output fusion | flops 9158656 | bytes 131072 | tf_op jit(solution)/shard_map/jit(cumsum)/reduce_window_sum | solution.py:78
  51.8 6.4 %fusion.35 = f32[16,2,128,512]{3,2,1,0:T(8,128)S(1)} fusion(f32[16,2,64,512]{3,2,1,0:T(8,128)} %param.10, s32[16,2,64]{2,1,0:T(2,128)S(1)} %copy.81, pred[16,2,64]{2,1,0:T(4,128)(4,1)S(1)} %copy.82), kind=kOutput, calls=%fused_computation.104 | convolution fusion | flops 1611137024 | bytes 12593152 | tf_op jit(solution)/shard_map/fcsq,fcqj->fcsj/dot_general | solution.py:89
  58.2 1.1 fusion.33
  59.4 1.1 fusion.32
  60.4 1.1 fusion.31
  61.5 1.0 fusion.30
  62.5 1.1 fusion.29
  63.7 1.0 fusion.28
  64.7 1.1 fusion.27
  65.8 1.1 fusion.26
  66.8 7.4 %all-to-all-start = ((f32[8,16,2,1,16,512]{5,4,2,1,3,0:T(8,128)}), f32[8,16,2,1,16,512]{5,4,2,1,3,0:T(8,128)}, u32[]{:S(2)}, u32[]{:S(2)}) async-start(f32[8,16,2,1,16,512]{5,4,2,1,3,0:T(8,128)} %fusion.26), calls=%async_computation | async-start | bytes 16777216 | tf_op jit(solution)/shard_map/all_to_all | solution.py:11
  74.5 6.0 fusion.19
  80.5 176.9 %all-to-all-done = f32[8,16,2,1,16,512]{5,4,2,1,3,0:T(8,128)} async-done(((f32[8,16,2,1,16,512]{5,4,2,1,3,0:T(8,128)}), f32[8,16,2,1,16,512]{5,4,2,1,3,0:T(8,128)}, u32[]{:S(2)}, u32[]{:S(2)}) %all-to-all-start) | async-done | bytes 8388640 | tf_op jit(solution)/shard_map/all_to_all | solution.py:11
  257.4 4.4 copy.90
  261.9 7.6 %fusion.69 = f32[16,2,96,512]{3,2,1,0:T(8,128)} fusion(f32[16,2,96,128]{3,2,1,0:T(8,128)S(1)} %fusion.19, f32[16,2,128,512]{3,2,1,0:T(8,128)S(1)} %bitcast.139), kind=kOutput, calls=%fused_computation.164 | convolution fusion | flops 2415919104 | bytes 16252928 | tf_op jit(solution)/shard_map/fclp,fcpq->fclq/dot_general | solution.py:99
  269.5 69.4 %while.33 = (s32[]{:T(128)}, f32[16,96,768]{2,1,0:T(8,128)}, f32[16,2,96,512]{3,2,1,0:T(8,128)}, s32[16,2,512]{2,1,0:T(2,128)S(1)}, s32[]{:T(128)}, /*index=5*/s32[]{:T(128)}, s32[]{}) while((s32[]{:T(128)}, f32[16,96,768]{2,1,0:T(8,128)}, f32[16,2,96,512]{3,2,1,0:T(8,128)}, s32[16,2,512]{2,1,0:T(2,128)S(1)}, s32[]{:T(128)}, ...), condition=%wide.region_3.4_spmd.clone, body=%wide.region_2.3_spmd.clone.sunk | while | flops 906829824 | bytes 2864737 | solution.py:112
  269.5 0.5 iota_compare_fusion.29
  270.0 1.6 fusion.89
  271.5 2.3 fusion.90
  274.3 1.6 fusion.89
  275.9 2.3 fusion.90
  278.6 1.6 fusion.89
  280.2 2.3 fusion.90
  283.0 1.6 fusion.89
  284.5 2.3 fusion.90
  287.3 1.6 fusion.89
  288.8 2.3 fusion.90
  291.6 1.6 fusion.89
  293.2 2.3 fusion.90
  296.0 1.6 fusion.89
  297.5 2.3 fusion.90
  300.3 1.6 fusion.89
  301.9 2.3 fusion.90
  304.7 1.6 fusion.89
  306.2 2.3 fusion.90
  309.0 1.6 fusion.89
  310.6 2.3 fusion.90
  313.3 1.6 fusion.89
  314.9 2.3 fusion.90
  317.7 1.6 fusion.89
  319.2 2.3 fusion.90
  322.0 1.6 fusion.89
  323.6 2.3 fusion.90
  326.3 1.6 fusion.89
  327.9 2.3 fusion.90
  330.7 1.6 fusion.89
  332.2 2.2 fusion.90
  335.0 1.6 fusion.89
  336.6 2.3 fusion.90
  338.8 1.6 slice_add_fusion.1
  340.4 3.6 all-to-all-start.1
  344.4 7.0 %all-to-all-done.1 = f32[16,16,128]{2,1,0:T(8,128)S(1)} async-done(((f32[16,16,128]{2,1,0:T(8,128)}), f32[16,16,128]{2,1,0:T(8,128)S(1)}, u32[]{:S(2)}, u32[]{:S(2)}) %all-to-all-start.1) | async-done | bytes 131104 | tf_op jit(solution)/shard_map/all_to_all | solution.py:117
  351.5 83.5 %while.34 = (s32[]{:T(128)}, f32[2,128,128]{1,2,0:T(8,128)S(1)}, f32[2,128,128]{1,2,0:T(8,128)S(1)}, f32[2,128]{1,0:T(2,128)S(1)}, s32[]{:T(128)}, /*index=5*/s3...) while((s32[]{:T(128)}, f32[2,128,128]{1,2,0:T(8,128)S(1)}, ...), condition=%wide.region_5.6_spmd.clone.clone, body=%wide.region_4.5_spmd.clone.clone.sunk | while | flops 3349669 | bytes 1026329 | solution.py:50
  435.1 19.7 %custom-call.4 = f32[2,1,128,128]{2,3,1,0:T(8,128)S(1)} custom-call(f32[2,1,128,128]{3,2,1,0:T(8,128)S(1)} %add_bitcast_fusion), custom_call_target="InvertDiagBlocksLowerTriangular" | custom-call | tf_op jit(solution)/shard_map/vmap(jit(_solve_triangular))/triangular_solve | solution.py:53
  454.8 1.0 fusion.43
  455.9 5.8 slice_add_fusion
  461.7 32.6 %all-gather.4.cloned.1.call-done = f32[16,128,128]{2,1,0:T(8,128)} async-done(((f32[2,128,128]{2,1,0:T(8,128)}), f32[16,128,128]{2,1,0:T(8,128)}) %all-gather.4.cloned.1.call-update) | async-done | bytes 1048592 | tf_op jit(solution)/shard_map/all_gather | solution.py:120
  494.3 4.4 fusion.37
  498.8 18.7 %all-gather = f32[8,2,128]{2,1,0:T(2,128)S(1)} all-gather(f32[1,2,128]{2,1,0:T(2,128)S(1)} %bitcast.172), channel_id=1, replica_groups=mesh['row'=8,'col'=4] {'row'}, dimensions={0}, use_global_device_ids=true | all-gather | bytes 9216 | tf_op jit(solution)/shard_map/all_gather | solution.py:121
  517.5 0.6 select_reduce_fusion
  518.1 6.7 %psum.7 = f32[]{:T(128)} all-reduce(f32[]{:T(128)} %select_reduce_fusion), channel_id=1, replica_groups=mesh['row'=8,'col'=4] {'col'}, use_global_device_ids=true, to_apply=%region_7.8 | all-reduce | flops 1 | bytes 8 | tf_op jit(solution)/shard_map/psum | solution.py:130
  525.4 58.1 %all-gather.6.cloned.1.call-done = f32[16,640,128]{2,1,0:T(8,128)} async-done(((f32[16,80,128]{2,1,0:T(8,128)}), f32[16,640,128]{2,1,0:T(8,128)}) %all-gather.6.cloned.1.call-update) | async-done | bytes 5242896 | tf_op jit(solution)/shard_map/all_gather | solution.py:126
  583.5 11.6 %slice_subtract_fusion = f32[16,80,640]{2,1,0:T(8,128)} fusion(f32[16,80,768]{2,1,0:T(8,128)} %slice_add_fusion, f32[16,640,128]{2,1,0:T(8,128)} %all-gather.6.cloned.1.call-done, f32[16,80,128]{2,1,0:T(8,128)} %fusion.37, f32[16,128]{1,0:T(8,128)S(1)} %bitcast.171), kind=kOutput, calls=%fused_computation.83 | convolution fusion | flops 1259274240 | bytes 12460032 | tf_op jit(solution)/shard_map/fik,fjk->fij/dot_general | solution.py:125
  (831 shorter events, 90.0 us)
Async XLA Ops:
  66.8 7.5 %copy-start = (s32[16,2,512]{2,1,0:T(2,128)S(1)}, s32[16,2,512]{2,1,0:T(2,128)}, u32[]{:S(2)}) copy-start(s32[16,2,512]{2,1,0:T(2,128)} %param.11) | copy-start | bytes 196612
  66.8 190.6 %all-to-all-start = ((f32[8,16,2,1,16,512]{5,4,2,1,3,0:T(8,128)}), f32[8,16,2,1,16,512]{5,4,2,1,3,0:T(8,128)}, u32[]{:S(2)}, u32[]{:S(2)}) async-start(f32[8,16,2,1,16,512]{5,4,2,1,3,0:T(8,128)} %fusion.26), calls=%async_computation | async-start | bytes 16777216 | tf_op jit(solution)/shard_map/all_to_all | solution.py:11
  269.4 69.4 %copy-start.1 = (f32[16,16,128]{2,1,0:T(8,128)S(1)}, f32[16,16,128]{2,1,0:T(8,128)}, u32[]{:S(2)}) copy-start(f32[16,16,128]{2,1,0:T(8,128)} %param.8) | copy-start | bytes 393220
  340.4 11.0 %all-to-all-start.1 = ((f32[16,16,128]{2,1,0:T(8,128)}), f32[16,16,128]{2,1,0:T(8,128)S(1)}, u32[]{:S(2)}, u32[]{:S(2)}) async-start(f32[16,16,128]{2,1,0:T(8,128)} %slice_add_fusion.1), calls=%async_computation.1 | async-start | bytes 262144 | tf_op jit(solution)/shard_map/all_to_all | solution.py:117
  344.0 150.3 %all-gather.4.cloned.1.call-start = ((), (), s32[]{:S(2)}) async-start(), calls=%async_computation.2 | async-start | bytes 1179648 | tf_op jit(solution)/shard_map/all_gather | solution.py:120
  455.9 127.7 %all-gather.6.cloned.1.call-start = ((), (), s32[]{:S(2)}) async-start(), calls=%async_computation.3 | async-start | bytes 5898240 | tf_op jit(solution)/shard_map/all_gather | solution.py:126
Sparse Core Ops, SparseCore 0:
  456.0 38.2 all-gather.3
  498.9 84.6 all-gather.5
